TPU v7x, 32 devices: a whole 2x2x4 slice. The times are simulated.
32 devices in a mesh: dp: 2 (over core), section: 4 (over z), mp: 4 (over y, x).
Axes of the slice: x: 2, y: 2, z: 4, core: 2. Of those that a mesh axis runs over, the one named last changes fastest.
Arguments:
- inputs: bfloat16 [48, 512], P(('dp', 'mp')), may hold values from -6 to 6
- tangents: bfloat16 [48, 32, 512], P(('dp', 'mp')), may hold values from -6 to 6
- targets: bfloat16 [48, 1024], P(('dp', 'mp')), may hold values from -24 to 24
- target_jac: bfloat16 [48, 32, 1024], P(('dp', 'mp')), may hold values from -24 to 24
- rank_mask: int32 [48, 32], P(('dp', 'mp')), may hold values from 0 to 1, as said below
- batch_order: int32 [8, 6], P(('dp', 'mp')), may hold values from 0 to 5, each once within a row
- encoder: bfloat16 [512, 2048], replicated, may hold values from -0.25 to 0.25
- layers: bfloat16 [4, 2048, 2048], P('section', 'mp'), may hold values from -0.125 to 0.125
- head_weight: bfloat16 [2048, 1024], replicated, may hold values from -0.125 to 0.125
Outputs:
- grad_layers: float32 [4, 2048, 2048], P('section', ('dp', 'mp'))
- grad_head: float32 [2048, 1024], P(('dp', 'mp'), 'section')
- loss_value: float32 [], replicated
Inputs may be any that keep to these rules, and one draw needn't show every extreme that they name: `rank_mask`: each sample's ones are its first 1 to 32 directions. `batch_order`: each row is an ordering of 0 .. 5.
All inputs are finite; a program needn't handle non-finite values.
Results may differ from a plain program's by a relative error of at most 0.035.
Values may be sent and summed in bfloat16 or wider, within the bound.
No kernel may reach another device: no remote copies, remote signals or barrier semaphores. Data moves between devices by JAX's collectives and lax.ppermute only.
A program may use at most 128 MiB of HBM per device.

v0:
```python
import jax
import jax.numpy as jnp
from jax import lax
from jax.sharding import PartitionSpec as P

MB = 6


def from_behind(value, axis, steps):
    count = lax.axis_size(axis)
    initial, last = (max(0, -steps), min(count, count - steps))
    return lax.ppermute(value, axis, [(source, source + steps) for source in range(initial, last)])


def forward_layer(row_block, weight):
    model_width = weight.shape[1]
    pre_act = jnp.dot(
        row_block.reshape(-1, model_width), weight, preferred_element_type=jnp.float32
    ).reshape(row_block.shape)
    tanh_p = jnp.tanh(pre_act[:, 0])
    slope_vals = 1.0 - tanh_p * tanh_p
    primal = row_block[:, 0].astype(jnp.float32) + tanh_p
    tangent = row_block[:, 1:].astype(jnp.float32) + slope_vals[:, None, :] * pre_act[:, 1:]
    return (jnp.concatenate([primal[:, None], tangent], axis=1).astype(jnp.bfloat16), pre_act)


def backward_layer(pre_act, grad_rows, weight):
    model_width = weight.shape[1]
    upstream = grad_rows.astype(jnp.float32)
    tanh_p = jnp.tanh(pre_act[:, 0])
    slope_vals = 1.0 - tanh_p * tanh_p
    tangent_part = upstream[:, 1:] * slope_vals[:, None, :]
    slope_grad = jnp.sum(upstream[:, 1:] * pre_act[:, 1:], axis=1)
    primal_part = upstream[:, 0] * slope_vals - 2.0 * slope_grad * tanh_p * slope_vals
    grad_mix = jnp.concatenate([primal_part[:, None], tangent_part], axis=1).astype(jnp.bfloat16)
    back_rows = jnp.dot(
        grad_mix.reshape(-1, model_width), weight.T, preferred_element_type=jnp.float32
    ).reshape(upstream.shape)
    return (grad_mix, (upstream + back_rows).astype(jnp.bfloat16))


def place_slot(store, value, batch_slot, is_valid):
    return lax.dynamic_update_index_in_dim(
        store, jnp.where(is_valid, value, store[batch_slot]), batch_slot, 0
    )


def local(
    inputs, tangents, targets, target_jac, rank_mask, batch_order, encoder, layers, head_weight
):
    samp_dev = inputs.shape[0]
    per_batch = samp_dev // MB
    row_depth = tangents.shape[1] + 1
    in_width = inputs.shape[1]
    model_width = layers.shape[2]
    out_width = head_weight.shape[1]
    sections = lax.axis_size("section")
    section_id = lax.axis_index("section")
    is_first = section_id == 0
    is_last = section_id == sections - 1
    layer_full = lax.all_gather(layers[0], "mp", axis=0, tiled=True)
    sample_order = batch_order[0]
    row_weight = jnp.concatenate(
        [jnp.ones((samp_dev, 1), jnp.float32), rank_mask.astype(jnp.float32)], axis=1
    )
    sample_total = jnp.sum(row_weight, axis=1)
    batch_counts = lax.psum(
        jnp.sum(sample_total[sample_order].reshape(MB, per_batch), axis=1), "mp"
    )

    def picked_of(batch_slot):
        return lax.dynamic_slice_in_dim(sample_order, batch_slot * per_batch, per_batch)

    def lift_batch(batch_slot):
        picked = picked_of(batch_slot)
        rows_in = jnp.concatenate([inputs[picked][:, None, :], tangents[picked]], axis=1)
        lifted = jnp.dot(rows_in.reshape(-1, in_width), encoder, preferred_element_type=jnp.float32)
        return lifted.reshape(per_batch, row_depth, model_width).astype(jnp.bfloat16)

    block_shape = (MB, per_batch, row_depth, model_width)
    pre_shape = (1, 1, 1, 1)

    def forward_tick(step_index, loop_state):
        incoming, store_in, store_pre, store_out = loop_state
        batch_index = step_index - section_id
        is_valid = (batch_index >= 0) & (batch_index < MB)
        batch_slot = jnp.clip(batch_index, 0, MB - 1)
        row_block = lax.cond(is_first, lambda: lift_batch(batch_slot), lambda: incoming)

        def forward_active():
            return forward_layer(row_block, layer_full)

        def forward_resting():
            return (row_block, jnp.zeros(row_block.shape, jnp.float32))

        layer_out, pre_act = lax.cond(is_valid, forward_active, forward_resting)
        store_in = place_slot(store_in, row_block, batch_slot, is_valid)
        store_out = place_slot(store_out, layer_out, batch_slot, is_valid)
        passed = from_behind(layer_out, "section", 1)
        return (passed, store_in, store_pre, store_out)

    start_state = (
        jnp.zeros(block_shape[1:], jnp.bfloat16),
        jnp.zeros(block_shape, jnp.bfloat16),
        jnp.zeros(pre_shape, jnp.float32),
        jnp.zeros(block_shape, jnp.bfloat16),
    )
    _, store_in, store_pre, store_out = lax.fori_loop(
        0, MB + sections - 1, forward_tick, start_state
    )

    def backward_tick(step_index, loop_state):
        incoming, store_mix, store_head, loss_acc = loop_state
        batch_index = step_index - (sections - 1 - section_id)
        is_valid = (batch_index >= 0) & (batch_index < MB)
        batch_slot = jnp.clip(batch_index, 0, MB - 1)
        batch_total = batch_counts[batch_slot]

        def head_part():
            final_rows = store_out[batch_slot]
            outputs = jnp.dot(
                final_rows.reshape(-1, model_width), head_weight, preferred_element_type=jnp.float32
            )
            outputs = outputs.reshape(per_batch, row_depth, out_width)
            picked = picked_of(batch_slot)
            wanted = jnp.concatenate(
                [targets[picked][:, None, :], target_jac[picked]], axis=1
            ).astype(jnp.float32)
            weights_here = row_weight[picked]
            mismatch = outputs - wanted
            misfit = jnp.sum(weights_here[:, :, None] * mismatch * mismatch) / batch_total
            cot_out = (2.0 * weights_here[:, :, None] * mismatch / batch_total).astype(jnp.bfloat16)
            grad_rows = jnp.dot(
                cot_out.reshape(-1, out_width), head_weight.T, preferred_element_type=jnp.float32
            )
            return (
                grad_rows.reshape(per_batch, row_depth, model_width).astype(jnp.bfloat16),
                cot_out,
                misfit,
            )

        def pass_on():
            return (
                incoming,
                jnp.zeros((per_batch, row_depth, out_width), jnp.bfloat16),
                jnp.zeros((), jnp.float32),
            )

        grad_rows, cot_out, misfit = lax.cond(is_last & is_valid, head_part, pass_on)

        def backward_active():
            row_block = store_in[batch_slot]
            pre_act = jnp.dot(
                row_block.reshape(-1, model_width), layer_full, preferred_element_type=jnp.float32
            ).reshape(row_block.shape)
            return backward_layer(pre_act, grad_rows, layer_full)

        def backward_resting():
            return (jnp.zeros(grad_rows.shape, jnp.bfloat16), grad_rows)

        grad_mix, grad_in = lax.cond(is_valid, backward_active, backward_resting)
        store_mix = place_slot(store_mix, grad_mix, batch_slot, is_valid)
        store_head = place_slot(store_head, cot_out, batch_slot, is_valid)
        loss_acc = loss_acc + jnp.where(is_valid, misfit, jnp.zeros((), jnp.float32))
        passed = from_behind(grad_in, "section", -1)
        return (passed, store_mix, store_head, loss_acc)

    back_state = (
        jnp.zeros(block_shape[1:], jnp.bfloat16),
        jnp.zeros(block_shape, jnp.bfloat16),
        jnp.zeros((MB, per_batch, row_depth, out_width), jnp.bfloat16),
        jnp.zeros((), jnp.float32),
    )
    _, store_mix, store_head, loss_acc = lax.fori_loop(
        0, MB + sections - 1, backward_tick, back_state
    )
    shard_rows = model_width // (lax.axis_size("dp") * lax.axis_size("mp"))
    in_flat = store_in.reshape(-1, model_width)
    mix_flat = store_mix.reshape(-1, model_width)
    grad_layers = lax.psum_scatter(
        jnp.dot(in_flat.T, mix_flat, preferred_element_type=jnp.float32).astype(jnp.bfloat16),
        ("dp", "mp"),
        scatter_dimension=0,
        tiled=True,
    ).astype(jnp.float32)[None]
    out_flat = store_out.reshape(-1, model_width)
    head_flat = store_head.reshape(-1, out_width)

    def compute():
        return jnp.dot(out_flat.T, head_flat, preferred_element_type=jnp.float32)

    def skipped():
        return jnp.zeros((lax.axis_size(("dp", "mp")) * shard_rows, out_width), jnp.float32)

    summed = lax.psum_scatter(
        lax.cond(is_last, compute, skipped).astype(jnp.bfloat16),
        ("dp", "mp"),
        scatter_dimension=0,
        tiled=True,
    )
    section_loss = lax.psum(loss_acc, ("dp", "mp"))
    loss_row = jnp.broadcast_to(section_loss, (1, sections))
    grad_head, loss_cols = (
        lax.psum_scatter(summed, "section", scatter_dimension=1, tiled=True).astype(jnp.float32),
        lax.psum_scatter(
            loss_row.astype(jnp.bfloat16), "section", scatter_dimension=1, tiled=True
        ).astype(jnp.float32),
    )
    loss_value = loss_cols[0, 0] / (lax.axis_size("dp") * MB * out_width)
    return (grad_layers, grad_head, loss_value)


def solution(mesh):
    in_specs = (
        P(("dp", "mp"), None),
        P(("dp", "mp"), None, None),
        P(("dp", "mp"), None),
        P(("dp", "mp"), None, None),
        P(("dp", "mp"), None),
        P(("dp", "mp"), None),
        P(),
        P("section", "mp", None),
        P(),
    )
    out_specs = (P("section", ("dp", "mp"), None), P(("dp", "mp"), "section"), P())
    return jax.shard_map(local, mesh=mesh, in_specs=in_specs, out_specs=out_specs, check_vma=False)
```

profile of v0, /device:TPU:0, one launch (start us, length us, event | category | flops | bytes accessed | tf_op | source)
XLA Modules:
  0.0 592.0 jit_solution(11319766208716329196)
XLA Ops:
  10.2 11.4 %psum.14 = f32[6]{0:T(128)S(1)} all-reduce(f32[6]{0:T(128)S(1)} %gather_fusion), channel_id=1, replica_groups=mesh['dp'=2,'section'=4,'mp'=4] {'mp'}, use_global_device_ids=true, to_apply=%region_7.0 | all-reduce | flops 6 | bytes 48 | tf_op jit(solution)/shard_map/psum | solution.py:67
  21.5 78.5 %all-gather.3.cloned.1.call-done = bf16[1,2048,2048]{2,1,0:T(8,128)(2,1)} async-done(((bf16[1,512,2048]{2,1,0:T(8,128)(2,1)}), bf16[1,2048,2048]{2,1,0:T(8,128)(2,1)}) %all-gather.3.cloned.1.call-update) | async-done | bytes 8388624 | tf_op jit(solution)/shard_map/all_gather | solution.py:61
  101.9 119.8 %while.49 = (s32[]{:T(128)}, bf16[1,33,2048]{2,1,0:T(8,128)(2,1)}, bf16[6,1,33,2048]{3,2,1,0:T(8,128)(2,1)S(1)}, bf16[6,1,33,2048]{3,2,1,0:T(8,128)(2,1)}, s32[]...) while((s32[]{:T(128)}, bf16[1,33,2048]{2,1,0:T(8,128)(2,1)}, ...), condition=%wide.region_5.0_spmd, body=%wide.region_0.5_spmd.sunk | while | flops 346843136 | bytes 14290849 | solution.py:108
  194.4 6.0 %collective-permute-start = (bf16[1,33,2048]{2,1,0:T(8,128)(2,1)S(1)}, bf16[1,33,2048]{2,1,0:T(8,128)(2,1)}, u32[]{:S(2)}, u32[]{:S(2)}) collective-permute-start(bf16[1,33,2048]{2,1,0:T(8,128)(2,1)S(1)} %get-tuple-element.1090), channel_id=1, source_target_pairs={{0,4},{4,8},{8,12},{1,5},{5,9},{9,13},{2,6},{6,10},{10,14},{3,7},{... | collective-permute-start | bytes 405512 | tf_op jit(solution)/shard_map/while/body/eval_jaxpr/ppermute | solution.py:12
  221.9 212.5 %while.50 = (s32[]{:T(128)}, bf16[1,33,2048]{2,1,0:T(8,128)(2,1)S(1)}, bf16[6,1,33,2048]{3,2,1,0:T(8,128)(2,1)S(1)}, bf16[6,1,33,1024]{3,2,1,0:T(8,128)(2,1)S(1)...) while((s32[]{:T(128)}, ...), condition=%wide.region_15.16_spmd, body=%wide.region_8.15_spmd.sunk | while | flops 832231424 | bytes 80709456 | solution.py:174
  224.1 6.3 %collective-permute-done.1 = bf16[1,33,2048]{2,1,0:T(8,128)(2,1)S(1)} collective-permute-done((bf16[1,33,2048]{2,1,0:T(8,128)(2,1)S(1)}, bf16[1,33,2048]{2,1,0:T(8,128)(2,1)S(1)}, u32[]{:S(2)}, u32[]{:S(2)}) %collective-permute-start.1) | collective-permute-done | bytes 135200 | tf_op jit(solution)/shard_map/while/body/eval_jaxpr/ppermute | solution.py:12
  232.6 8.7 %collective-permute-done.1 = bf16[1,33,2048]{2,1,0:T(8,128)(2,1)S(1)} collective-permute-done((bf16[1,33,2048]{2,1,0:T(8,128)(2,1)S(1)}, bf16[1,33,2048]{2,1,0:T(8,128)(2,1)S(1)}, u32[]{:S(2)}, u32[]{:S(2)}) %collective-permute-start.1) | collective-permute-done | bytes 135200 | tf_op jit(solution)/shard_map/while/body/eval_jaxpr/ppermute | solution.py:12
  243.4 43.9 %collective-permute-done.1 = bf16[1,33,2048]{2,1,0:T(8,128)(2,1)S(1)} collective-permute-done((bf16[1,33,2048]{2,1,0:T(8,128)(2,1)S(1)}, bf16[1,33,2048]{2,1,0:T(8,128)(2,1)S(1)}, u32[]{:S(2)}, u32[]{:S(2)}) %collective-permute-start.1) | collective-permute-done | bytes 135200 | tf_op jit(solution)/shard_map/while/body/eval_jaxpr/ppermute | solution.py:12
  288.0 8.5 %conditional.13 = (bf16[1,33,2048]{2,1,0:T(8,128)(2,1)S(1)}, bf16[1,33,2048]{2,1,0:T(8,128)(2,1)S(1)}) conditional(s32[]{:T(128)} %convert_element_type.140, bf16[1,33,2048]{2,1,0:T(8,128)(2,1)S(1)} %get-tuple-element.965, (bf16[1,33,2048]{2,1,0:T(8,128)(2,1)S(1)}, s32[]{:T(128)}, bf16[6,1,33,2048]{3,2,1,0:T(8,128)(2,1)S(1)}, ...), branch_computations={%region_12.12_spmd, %region_13.14_spmd} | conditional | flops 554866688 | bytes 53235792 | solution.py:161
  298.8 14.7 %collective-permute-done.1 = bf16[1,33,2048]{2,1,0:T(8,128)(2,1)S(1)} collective-permute-done((bf16[1,33,2048]{2,1,0:T(8,128)(2,1)S(1)}, bf16[1,33,2048]{2,1,0:T(8,128)(2,1)S(1)}, u32[]{:S(2)}, u32[]{:S(2)}) %collective-permute-start.1) | collective-permute-done | bytes 135200 | tf_op jit(solution)/shard_map/while/body/eval_jaxpr/ppermute | solution.py:12
  314.1 8.5 %conditional.13 = (bf16[1,33,2048]{2,1,0:T(8,128)(2,1)S(1)}, bf16[1,33,2048]{2,1,0:T(8,128)(2,1)S(1)}) conditional(s32[]{:T(128)} %convert_element_type.140, bf16[1,33,2048]{2,1,0:T(8,128)(2,1)S(1)} %get-tuple-element.965, (bf16[1,33,2048]{2,1,0:T(8,128)(2,1)S(1)}, s32[]{:T(128)}, bf16[6,1,33,2048]{3,2,1,0:T(8,128)(2,1)S(1)}, ...), branch_computations={%region_12.12_spmd, %region_13.14_spmd} | conditional | flops 554866688 | bytes 53235792 | solution.py:161
  325.0 14.7 %collective-permute-done.1 = bf16[1,33,2048]{2,1,0:T(8,128)(2,1)S(1)} collective-permute-done((bf16[1,33,2048]{2,1,0:T(8,128)(2,1)S(1)}, bf16[1,33,2048]{2,1,0:T(8,128)(2,1)S(1)}, u32[]{:S(2)}, u32[]{:S(2)}) %collective-permute-start.1) | collective-permute-done | bytes 135200 | tf_op jit(solution)/shard_map/while/body/eval_jaxpr/ppermute | solution.py:12
  340.3 8.5 %conditional.13 = (bf16[1,33,2048]{2,1,0:T(8,128)(2,1)S(1)}, bf16[1,33,2048]{2,1,0:T(8,128)(2,1)S(1)}) conditional(s32[]{:T(128)} %convert_element_type.140, bf16[1,33,2048]{2,1,0:T(8,128)(2,1)S(1)} %get-tuple-element.965, (bf16[1,33,2048]{2,1,0:T(8,128)(2,1)S(1)}, s32[]{:T(128)}, bf16[6,1,33,2048]{3,2,1,0:T(8,128)(2,1)S(1)}, ...), branch_computations={%region_12.12_spmd, %region_13.14_spmd} | conditional | flops 554866688 | bytes 53235792 | solution.py:161
  351.1 14.7 %collective-permute-done.1 = bf16[1,33,2048]{2,1,0:T(8,128)(2,1)S(1)} collective-permute-done((bf16[1,33,2048]{2,1,0:T(8,128)(2,1)S(1)}, bf16[1,33,2048]{2,1,0:T(8,128)(2,1)S(1)}, u32[]{:S(2)}, u32[]{:S(2)}) %collective-permute-start.1) | collective-permute-done | bytes 135200 | tf_op jit(solution)/shard_map/while/body/eval_jaxpr/ppermute | solution.py:12
  366.4 8.5 %conditional.13 = (bf16[1,33,2048]{2,1,0:T(8,128)(2,1)S(1)}, bf16[1,33,2048]{2,1,0:T(8,128)(2,1)S(1)}) conditional(s32[]{:T(128)} %convert_element_type.140, bf16[1,33,2048]{2,1,0:T(8,128)(2,1)S(1)} %get-tuple-element.965, (bf16[1,33,2048]{2,1,0:T(8,128)(2,1)S(1)}, s32[]{:T(128)}, bf16[6,1,33,2048]{3,2,1,0:T(8,128)(2,1)S(1)}, ...), branch_computations={%region_12.12_spmd, %region_13.14_spmd} | conditional | flops 554866688 | bytes 53235792 | solution.py:161
  377.2 14.7 %collective-permute-done.1 = bf16[1,33,2048]{2,1,0:T(8,128)(2,1)S(1)} collective-permute-done((bf16[1,33,2048]{2,1,0:T(8,128)(2,1)S(1)}, bf16[1,33,2048]{2,1,0:T(8,128)(2,1)S(1)}, u32[]{:S(2)}, u32[]{:S(2)}) %collective-permute-start.1) | collective-permute-done | bytes 135200 | tf_op jit(solution)/shard_map/while/body/eval_jaxpr/ppermute | solution.py:12
  392.6 8.5 %conditional.13 = (bf16[1,33,2048]{2,1,0:T(8,128)(2,1)S(1)}, bf16[1,33,2048]{2,1,0:T(8,128)(2,1)S(1)}) conditional(s32[]{:T(128)} %convert_element_type.140, bf16[1,33,2048]{2,1,0:T(8,128)(2,1)S(1)} %get-tuple-element.965, (bf16[1,33,2048]{2,1,0:T(8,128)(2,1)S(1)}, s32[]{:T(128)}, bf16[6,1,33,2048]{3,2,1,0:T(8,128)(2,1)S(1)}, ...), branch_computations={%region_12.12_spmd, %region_13.14_spmd} | conditional | flops 554866688 | bytes 53235792 | solution.py:161
  403.4 14.7 %collective-permute-done.1 = bf16[1,33,2048]{2,1,0:T(8,128)(2,1)S(1)} collective-permute-done((bf16[1,33,2048]{2,1,0:T(8,128)(2,1)S(1)}, bf16[1,33,2048]{2,1,0:T(8,128)(2,1)S(1)}, u32[]{:S(2)}, u32[]{:S(2)}) %collective-permute-start.1) | collective-permute-done | bytes 135200 | tf_op jit(solution)/shard_map/while/body/eval_jaxpr/ppermute | solution.py:12
  418.7 8.5 %conditional.13 = (bf16[1,33,2048]{2,1,0:T(8,128)(2,1)S(1)}, bf16[1,33,2048]{2,1,0:T(8,128)(2,1)S(1)}) conditional(s32[]{:T(128)} %convert_element_type.140, bf16[1,33,2048]{2,1,0:T(8,128)(2,1)S(1)} %get-tuple-element.965, (bf16[1,33,2048]{2,1,0:T(8,128)(2,1)S(1)}, s32[]{:T(128)}, bf16[6,1,33,2048]{3,2,1,0:T(8,128)(2,1)S(1)}, ...), branch_computations={%region_12.12_spmd, %region_13.14_spmd} | conditional | flops 554866688 | bytes 53235792 | solution.py:161
  437.0 48.5 %reduce-scatter.7.cloned.1.call-done = bf16[256,1024]{1,0:T(8,128)(2,1)} async-done(((bf16[2048,1024]{1,0:T(8,128)(2,1)}), bf16[256,1024]{1,0:T(8,128)(2,1)}) %reduce-scatter.7.cloned.1.call-update) | async-done | bytes 524304 | tf_op jit(solution)/shard_map/reduce_scatter | solution.py:195
  485.7 5.6 bitcast_convert_fusion
  492.5 15.4 %psum.15 = bf16[]{:T(256)} all-reduce(f32[]{:T(128)} %get-tuple-element.664), channel_id=1, replica_groups=mesh['dp'=2,'section'=4,'mp'=4] {'dp','mp'}, use_global_device_ids=true, to_apply=%region_21.22 | all-reduce | flops 1 | bytes 6 | tf_op jit(solution)/shard_map/psum | solution.py:201
  508.6 12.1 %all-reduce.1 = bf16[1,4]{1,0:T(2,128)(2,1)S(1)} all-reduce(bf16[1,4]{1,0:T(2,128)(2,1)S(1)} %broadcast_in_dim.72), channel_id=6, replica_groups=mesh['dp'=2,'section'=4,'mp'=4] {'section'}, use_global_device_ids=true, to_apply=%region_22.23.clone | all-reduce | flops 4 | bytes 16
  523.6 59.1 %reduce-scatter.5.cloned.1.call-done = bf16[256,2048]{1,0:T(8,128)(2,1)} async-done(((bf16[2048,2048]{1,0:T(8,128)(2,1)}), bf16[256,2048]{1,0:T(8,128)(2,1)}) %reduce-scatter.5.cloned.1.call-update) | async-done | bytes 1048592 | tf_op jit(solution)/shard_map/reduce_scatter | solution.py:180
  (306 shorter events, 269.7 us)
Async XLA Ops:
  7.2 94.8 %copy-start.3 = (s32[1,6]{1,0:T(1,128)S(1)}, s32[1,6]{1,0:T(1,128)}, u32[]{:S(2)}) copy-start(s32[1,6]{1,0:T(1,128)} %param.28) | copy-start | bytes 76
  7.2 94.8 %copy-start.2 = (bf16[512,2048]{1,0:T(8,128)(2,1)S(1)}, bf16[512,2048]{1,0:T(8,128)(2,1)}, u32[]{:S(2)}) copy-start(bf16[512,2048]{1,0:T(8,128)(2,1)} %param.29) | copy-start | bytes 6291460
  7.2 92.9 %all-gather.3.cloned.1.call-start = ((), (), s32[]{:S(2)}) async-start(), calls=%async_computation.6 | async-start | bytes 10485760 | tf_op jit(solution)/shard_map/all_gather | solution.py:61
  7.9 477.5 %reduce-scatter.7.cloned.1.call-start = ((), (), s32[]{:S(2)}) async-start(), calls=%async_computation.4 | async-start | bytes 4718592 | tf_op jit(solution)/shard_map/reduce_scatter | solution.py:195
  112.2 4.9 collective-permute-start
  127.4 4.3 collective-permute-start
  141.9 4.1 collective-permute-start
  156.3 4.1 collective-permute-start
  170.7 4.1 collective-permute-start
  185.1 4.1 collective-permute-start
  194.4 8.1 %collective-permute-start = (bf16[1,33,2048]{2,1,0:T(8,128)(2,1)S(1)}, bf16[1,33,2048]{2,1,0:T(8,128)(2,1)}, u32[]{:S(2)}, u32[]{:S(2)}) collective-permute-start(bf16[1,33,2048]{2,1,0:T(8,128)(2,1)S(1)} %get-tuple-element.1090), channel_id=1, source_target_pairs={{0,4},{4,8},{8,12},{1,5},{5,9},{9,13},{2,6},{6,10},{10,14},{3,7},{... | collective-permute-start | bytes 405512 | tf_op jit(solution)/shard_map/while/body/eval_jaxpr/ppermute | solution.py:12
  207.8 4.1 collective-permute-start
  217.1 4.6 collective-permute-start
  222.6 7.8 %collective-permute-start.1 = (bf16[1,33,2048]{2,1,0:T(8,128)(2,1)S(1)}, bf16[1,33,2048]{2,1,0:T(8,128)(2,1)S(1)}, u32[]{:S(2)}, u32[]{:S(2)}) collective-permute-start(bf16[1,33,2048]{2,1,0:T(8,128)(2,1)S(1)} %get-tuple-element.966), channel_id=1, source_target_pairs={{4,0},{8,4},{12,8},{5,1},{9,5},{13,9},{6,2},{10,6},{14,10},{7,3},{... | collective-permute-start | bytes 405512 | tf_op jit(solution)/shard_map/while/body/eval_jaxpr/ppermute | solution.py:12
  231.1 10.2 %collective-permute-start.1 = (bf16[1,33,2048]{2,1,0:T(8,128)(2,1)S(1)}, bf16[1,33,2048]{2,1,0:T(8,128)(2,1)S(1)}, u32[]{:S(2)}, u32[]{:S(2)}) collective-permute-start(bf16[1,33,2048]{2,1,0:T(8,128)(2,1)S(1)} %get-tuple-element.966), channel_id=1, source_target_pairs={{4,0},{8,4},{12,8},{5,1},{9,5},{13,9},{6,2},{10,6},{14,10},{7,3},{... | collective-permute-start | bytes 405512 | tf_op jit(solution)/shard_map/while/body/eval_jaxpr/ppermute | solution.py:12
  242.0 45.4 %collective-permute-start.1 = (bf16[1,33,2048]{2,1,0:T(8,128)(2,1)S(1)}, bf16[1,33,2048]{2,1,0:T(8,128)(2,1)S(1)}, u32[]{:S(2)}, u32[]{:S(2)}) collective-permute-start(bf16[1,33,2048]{2,1,0:T(8,128)(2,1)S(1)} %get-tuple-element.966), channel_id=1, source_target_pairs={{4,0},{8,4},{12,8},{5,1},{9,5},{13,9},{6,2},{10,6},{14,10},{7,3},{... | collective-permute-start | bytes 405512 | tf_op jit(solution)/shard_map/while/body/eval_jaxpr/ppermute | solution.py:12
  296.5 17.0 %collective-permute-start.1 = (bf16[1,33,2048]{2,1,0:T(8,128)(2,1)S(1)}, bf16[1,33,2048]{2,1,0:T(8,128)(2,1)S(1)}, u32[]{:S(2)}, u32[]{:S(2)}) collective-permute-start(bf16[1,33,2048]{2,1,0:T(8,128)(2,1)S(1)} %get-tuple-element.966), channel_id=1, source_target_pairs={{4,0},{8,4},{12,8},{5,1},{9,5},{13,9},{6,2},{10,6},{14,10},{7,3},{... | collective-permute-start | bytes 405512 | tf_op jit(solution)/shard_map/while/body/eval_jaxpr/ppermute | solution.py:12
  322.6 17.0 %collective-permute-start.1 = (bf16[1,33,2048]{2,1,0:T(8,128)(2,1)S(1)}, bf16[1,33,2048]{2,1,0:T(8,128)(2,1)S(1)}, u32[]{:S(2)}, u32[]{:S(2)}) collective-permute-start(bf16[1,33,2048]{2,1,0:T(8,128)(2,1)S(1)} %get-tuple-element.966), channel_id=1, source_target_pairs={{4,0},{8,4},{12,8},{5,1},{9,5},{13,9},{6,2},{10,6},{14,10},{7,3},{... | collective-permute-start | bytes 405512 | tf_op jit(solution)/shard_map/while/body/eval_jaxpr/ppermute | solution.py:12
  348.8 17.0 %collective-permute-start.1 = (bf16[1,33,2048]{2,1,0:T(8,128)(2,1)S(1)}, bf16[1,33,2048]{2,1,0:T(8,128)(2,1)S(1)}, u32[]{:S(2)}, u32[]{:S(2)}) collective-permute-start(bf16[1,33,2048]{2,1,0:T(8,128)(2,1)S(1)} %get-tuple-element.966), channel_id=1, source_target_pairs={{4,0},{8,4},{12,8},{5,1},{9,5},{13,9},{6,2},{10,6},{14,10},{7,3},{... | collective-permute-start | bytes 405512 | tf_op jit(solution)/shard_map/while/body/eval_jaxpr/ppermute | solution.py:12
  374.9 17.0 %collective-permute-start.1 = (bf16[1,33,2048]{2,1,0:T(8,128)(2,1)S(1)}, bf16[1,33,2048]{2,1,0:T(8,128)(2,1)S(1)}, u32[]{:S(2)}, u32[]{:S(2)}) collective-permute-start(bf16[1,33,2048]{2,1,0:T(8,128)(2,1)S(1)} %get-tuple-element.966), channel_id=1, source_target_pairs={{4,0},{8,4},{12,8},{5,1},{9,5},{13,9},{6,2},{10,6},{14,10},{7,3},{... | collective-permute-start | bytes 405512 | tf_op jit(solution)/shard_map/while/body/eval_jaxpr/ppermute | solution.py:12
  401.1 17.0 %collective-permute-start.1 = (bf16[1,33,2048]{2,1,0:T(8,128)(2,1)S(1)}, bf16[1,33,2048]{2,1,0:T(8,128)(2,1)S(1)}, u32[]{:S(2)}, u32[]{:S(2)}) collective-permute-start(bf16[1,33,2048]{2,1,0:T(8,128)(2,1)S(1)} %get-tuple-element.966), channel_id=1, source_target_pairs={{4,0},{8,4},{12,8},{5,1},{9,5},{13,9},{6,2},{10,6},{14,10},{7,3},{... | collective-permute-start | bytes 405512 | tf_op jit(solution)/shard_map/while/body/eval_jaxpr/ppermute | solution.py:12
  427.2 7.2 %collective-permute-start.1 = (bf16[1,33,2048]{2,1,0:T(8,128)(2,1)S(1)}, bf16[1,33,2048]{2,1,0:T(8,128)(2,1)S(1)}, u32[]{:S(2)}, u32[]{:S(2)}) collective-permute-start(bf16[1,33,2048]{2,1,0:T(8,128)(2,1)S(1)} %get-tuple-element.966), channel_id=1, source_target_pairs={{4,0},{8,4},{12,8},{5,1},{9,5},{13,9},{6,2},{10,6},{14,10},{7,3},{... | collective-permute-start | bytes 405512 | tf_op jit(solution)/shard_map/while/body/eval_jaxpr/ppermute | solution.py:12
  436.9 85.0 %reduce-scatter.9.cloned.1.call-start = ((), (), s32[]{:S(2)}) async-start(), calls=%async_computation.5 | async-start | bytes 655360 | tf_op jit(solution)/shard_map/reduce_scatter | solution.py:204
  485.5 97.2 %reduce-scatter.5.cloned.1.call-start = ((), (), s32[]{:S(2)}) async-start(), calls=%async_computation.3 | async-start | bytes 9437184 | tf_op jit(solution)/shard_map/reduce_scatter | solution.py:180
  (7 other events, 35.3 us)
Sparse Core Ops, SparseCore 0:
  9.8 90.1 all-gather.2
  437.0 48.3 reduce-scatter.6
  487.7 21.8 reduce-scatter.8
  512.9 69.6 reduce-scatter.4
where the time goes:
time: 595 us; the launch traced here: 592 us
  waiting for transfers between devices  329 us (55%)
  matrix products  85.4 us (14%)
  local copies, waits for them, and re-layouts  51.3 us (9%)
  blocking collectives  38.9 us (7%)
  starting transfers between devices  34.3 us (6%)
  other arithmetic  22.6 us (4%)
  loops' own time  16.8 us (3%)
  between operations  13.8 us (2%)
    ppermute x18, waiting for transfers between devices, from_behind(): lax.ppermute(value, axis, [(source, source + steps) for source in range(i...  142 us
    all_gather x1, waiting for transfers between devices, local(): layer_full = lax.all_gather(layers[0], 'mp', axis=0, tiled=True)  78.5 us
    reduce_scatter x1, waiting for transfers between devices, local(): lax.psum_scatter(jnp.dot(in_flat.T, mix_flat, preferred_element_type=jnp....  59.1 us
    reduce_scatter x1, waiting for transfers between devices, local(): lax.psum_scatter(lax.cond(is_last, compute, skipped).astype(jnp.bfloat16)...  48.5 us
    ppermute x18, starting transfers between devices, from_behind(): lax.ppermute(value, axis, [(source, source + steps) for source in range(i...  33.9 us
    dot_general x6, matrix products, backward_active(): jnp.dot(row_block.reshape(-1, model_width), layer_full, preferred_element...  30.4 us
    dot_general x6, matrix products, forward_layer(): jnp.dot(row_block.reshape(-1, model_width), weight, preferred_element_typ...  29.5 us
    another operation x27, local copies, waits for them, and re-layouts  18.5 us
  transfers between devices with their start and end apart: 22, of which 21 were waited for; matrix products, arithmetic and copies ran while one was open for 6% of the time, Pallas kernels for 0%

commit v1 on v0

--- a/solution.py
+++ b/solution.py
@@ -58,7 +58,9 @@
     section_id = lax.axis_index("section")
     is_first = section_id == 0
     is_last = section_id == sections - 1
-    layer_full = lax.all_gather(layers[0], "mp", axis=0, tiled=True)
+    layer_full = jnp.concatenate(
+        lax.all_to_all(jnp.stack([layers[0]] * lax.axis_size("mp")), "mp", 0, 0), axis=0
+    )
     sample_order = batch_order[0]
     row_weight = jnp.concatenate(
         [jnp.ones((samp_dev, 1), jnp.float32), rank_mask.astype(jnp.float32)], axis=1

time: 595 us -> 638 us (1.072)
  blocking collectives: 38.9 us -> 124 us
  waiting for transfers between devices: 329 us -> 258 us
  matrix products: 85.4 us -> 105 us
    psum x1, blocking collectives: 11.4 us -> 96 us  [local(): lax.psum(jnp.sum(sample_total[sample_order].reshape(MB, per_batch), axis=...]
    all_gather x1 -> x0, waiting for transfers between devices: 78.5 us -> none  [local(): layer_full = lax.all_gather(layers[0], 'mp', axis=0, tiled=True)]
    dot_general x6, matrix products: 15.6 us -> 35.8 us  [backward_layer(): jnp.dot(grad_mix.reshape(-1, model_width), weight.T, preferred_element_ty...]
    ppermute x18, waiting for transfers between devices: 142 us -> 150 us  [from_behind(): lax.ppermute(value, axis, [(source, source + steps) for source in range(i...]
    another operation x27 -> x28, local copies, waits for them, and re-layouts: 18.5 us -> 24.4 us
  transfers between devices with their start and end apart: 22 -> 22, of which waited for: 21 -> 20; matrix products, arithmetic and copies ran while one was open for 6% -> 5% of each run, Pallas kernels for 0% -> 0%
where the time goes in v1:
time: 638 us; the launch traced here: 635 us
  waiting for transfers between devices  258 us (40%)
  blocking collectives  124 us (19%)
  matrix products  105 us (16%)
  local copies, waits for them, and re-layouts  54.9 us (9%)
  starting transfers between devices  40.3 us (6%)
  other arithmetic  21.3 us (3%)
  loops' own time  18.2 us (3%)
  between operations  13.8 us (2%)
    ppermute x18, waiting for transfers between devices, from_behind(): lax.ppermute(value, axis, [(source, source + steps) for source in range(i...  150 us
    psum x1, blocking collectives, local(): lax.psum(jnp.sum(sample_total[sample_order].reshape(MB, per_batch), axis=...  96 us
    reduce_scatter x1, waiting for transfers between devices, local(): lax.psum_scatter(jnp.dot(in_flat.T, mix_flat, preferred_element_type=jnp....  59.3 us
    reduce_scatter x1, waiting for transfers between devices, local(): lax.psum_scatter(lax.cond(is_last, compute, skipped).astype(jnp.bfloat16)...  48.6 us
    dot_general x6, matrix products, backward_layer(): jnp.dot(grad_mix.reshape(-1, model_width), weight.T, preferred_element_ty...  35.8 us
    ppermute x18, starting transfers between devices, from_behind(): lax.ppermute(value, axis, [(source, source + steps) for source in range(i...  34.2 us
    dot_general x6, matrix products, forward_layer(): jnp.dot(row_block.reshape(-1, model_width), weight, preferred_element_typ...  29.5 us
    dot_general x6, matrix products, backward_active(): jnp.dot(row_block.reshape(-1, model_width), layer_full, preferred_element...  29.5 us
  transfers between devices with their start and end apart: 22, of which 20 were waited for; matrix products, arithmetic and copies ran while one was open for 5% of the time, Pallas kernels for 0%

profile of v1, /device:TPU:0, one launch (start us, length us, event | category | flops | bytes accessed | tf_op | source)
XLA Modules:
  0.0 634.8 jit_solution(2145048887419913694)
XLA Ops:
  19.8 96.0 %psum.14 = f32[6]{0:T(128)S(1)} all-reduce(f32[6]{0:T(128)S(1)} %gather_fusion), channel_id=1, replica_groups=mesh['dp'=2,'section'=4,'mp'=4] {'mp'}, use_global_device_ids=true, to_apply=%region_7.0 | all-reduce | flops 6 | bytes 48 | tf_op jit(solution)/shard_map/psum | solution.py:69
  117.7 121.0 %while.49 = (s32[]{:T(128)}, bf16[1,33,2048]{2,1,0:T(8,128)(2,1)}, bf16[6,1,33,2048]{3,2,1,0:T(8,128)(2,1)S(1)}, bf16[6,1,33,2048]{3,2,1,0:T(8,128)(2,1)}, s32[]...) while((s32[]{:T(128)}, bf16[1,33,2048]{2,1,0:T(8,128)(2,1)}, ...), condition=%wide.region_5.0_spmd, body=%wide.region_0.5_spmd.sunk | while | flops 346843136 | bytes 14290849 | solution.py:110
  238.8 238.0 %while.50 = (s32[]{:T(128)}, bf16[1,33,2048]{2,1,0:T(8,128)(2,1)S(1)}, bf16[6,1,33,2048]{3,2,1,0:T(8,128)(2,1)S(1)}, bf16[6,1,33,1024]{3,2,1,0:T(8,128)(2,1)S(1)...) while((s32[]{:T(128)}, ...), condition=%wide.region_15.16_spmd, body=%wide.region_8.15_spmd.sunk | while | flops 832231424 | bytes 47154988 | solution.py:176
  241.0 6.8 %collective-permute-done.1 = bf16[1,33,2048]{2,1,0:T(8,128)(2,1)S(1)} collective-permute-done((bf16[1,33,2048]{2,1,0:T(8,128)(2,1)S(1)}, bf16[1,33,2048]{2,1,0:T(8,128)(2,1)S(1)}, u32[]{:S(2)}, u32[]{:S(2)}) %collective-permute-start.1) | collective-permute-done | bytes 135200 | tf_op jit(solution)/shard_map/while/body/eval_jaxpr/ppermute | solution.py:12
  250.0 7.4 %collective-permute-done.1 = bf16[1,33,2048]{2,1,0:T(8,128)(2,1)S(1)} collective-permute-done((bf16[1,33,2048]{2,1,0:T(8,128)(2,1)S(1)}, bf16[1,33,2048]{2,1,0:T(8,128)(2,1)S(1)}, u32[]{:S(2)}, u32[]{:S(2)}) %collective-permute-start.1) | collective-permute-done | bytes 135200 | tf_op jit(solution)/shard_map/while/body/eval_jaxpr/ppermute | solution.py:12
  259.5 52.5 %collective-permute-done.1 = bf16[1,33,2048]{2,1,0:T(8,128)(2,1)S(1)} collective-permute-done((bf16[1,33,2048]{2,1,0:T(8,128)(2,1)S(1)}, bf16[1,33,2048]{2,1,0:T(8,128)(2,1)S(1)}, u32[]{:S(2)}, u32[]{:S(2)}) %collective-permute-start.1) | collective-permute-done | bytes 135200 | tf_op jit(solution)/shard_map/while/body/eval_jaxpr/ppermute | solution.py:12
  312.6 11.2 %conditional.13 = (bf16[1,33,2048]{2,1,0:T(8,128)(2,1)S(1)}, bf16[1,33,2048]{2,1,0:T(8,128)(2,1)S(1)}) conditional(s32[]{:T(128)} %convert_element_type.140, bf16[1,33,2048]{2,1,0:T(8,128)(2,1)S(1)} %get-tuple-element.965, (bf16[1,33,2048]{2,1,0:T(8,128)(2,1)S(1)}, s32[]{:T(128)}, bf16[6,1,33,2048]{3,2,1,0:T(8,128)(2,1)S(1)}, ...), branch_computations={%region_12.12_spmd, %region_13.14_spmd} | conditional | flops 554866688 | bytes 19681334 | solution.py:163
  317.7 6.0 fusion.4
  326.1 15.0 %collective-permute-done.1 = bf16[1,33,2048]{2,1,0:T(8,128)(2,1)S(1)} collective-permute-done((bf16[1,33,2048]{2,1,0:T(8,128)(2,1)S(1)}, bf16[1,33,2048]{2,1,0:T(8,128)(2,1)S(1)}, u32[]{:S(2)}, u32[]{:S(2)}) %collective-permute-start.1) | collective-permute-done | bytes 135200 | tf_op jit(solution)/shard_map/while/body/eval_jaxpr/ppermute | solution.py:12
  341.7 11.2 %conditional.13 = (bf16[1,33,2048]{2,1,0:T(8,128)(2,1)S(1)}, bf16[1,33,2048]{2,1,0:T(8,128)(2,1)S(1)}) conditional(s32[]{:T(128)} %convert_element_type.140, bf16[1,33,2048]{2,1,0:T(8,128)(2,1)S(1)} %get-tuple-element.965, (bf16[1,33,2048]{2,1,0:T(8,128)(2,1)S(1)}, s32[]{:T(128)}, bf16[6,1,33,2048]{3,2,1,0:T(8,128)(2,1)S(1)}, ...), branch_computations={%region_12.12_spmd, %region_13.14_spmd} | conditional | flops 554866688 | bytes 19681334 | solution.py:163
  346.9 6.0 fusion.4
  355.3 15.0 %collective-permute-done.1 = bf16[1,33,2048]{2,1,0:T(8,128)(2,1)S(1)} collective-permute-done((bf16[1,33,2048]{2,1,0:T(8,128)(2,1)S(1)}, bf16[1,33,2048]{2,1,0:T(8,128)(2,1)S(1)}, u32[]{:S(2)}, u32[]{:S(2)}) %collective-permute-start.1) | collective-permute-done | bytes 135200 | tf_op jit(solution)/shard_map/while/body/eval_jaxpr/ppermute | solution.py:12
  370.9 11.2 %conditional.13 = (bf16[1,33,2048]{2,1,0:T(8,128)(2,1)S(1)}, bf16[1,33,2048]{2,1,0:T(8,128)(2,1)S(1)}) conditional(s32[]{:T(128)} %convert_element_type.140, bf16[1,33,2048]{2,1,0:T(8,128)(2,1)S(1)} %get-tuple-element.965, (bf16[1,33,2048]{2,1,0:T(8,128)(2,1)S(1)}, s32[]{:T(128)}, bf16[6,1,33,2048]{3,2,1,0:T(8,128)(2,1)S(1)}, ...), branch_computations={%region_12.12_spmd, %region_13.14_spmd} | conditional | flops 554866688 | bytes 19681334 | solution.py:163
  384.5 15.0 %collective-permute-done.1 = bf16[1,33,2048]{2,1,0:T(8,128)(2,1)S(1)} collective-permute-done((bf16[1,33,2048]{2,1,0:T(8,128)(2,1)S(1)}, bf16[1,33,2048]{2,1,0:T(8,128)(2,1)S(1)}, u32[]{:S(2)}, u32[]{:S(2)}) %collective-permute-start.1) | collective-permute-done | bytes 135200 | tf_op jit(solution)/shard_map/while/body/eval_jaxpr/ppermute | solution.py:12
  400.1 11.2 %conditional.13 = (bf16[1,33,2048]{2,1,0:T(8,128)(2,1)S(1)}, bf16[1,33,2048]{2,1,0:T(8,128)(2,1)S(1)}) conditional(s32[]{:T(128)} %convert_element_type.140, bf16[1,33,2048]{2,1,0:T(8,128)(2,1)S(1)} %get-tuple-element.965, (bf16[1,33,2048]{2,1,0:T(8,128)(2,1)S(1)}, s32[]{:T(128)}, bf16[6,1,33,2048]{3,2,1,0:T(8,128)(2,1)S(1)}, ...), branch_computations={%region_12.12_spmd, %region_13.14_spmd} | conditional | flops 554866688 | bytes 19681334 | solution.py:163
  405.2 6.0 fusion.4
  413.6 15.0 %collective-permute-done.1 = bf16[1,33,2048]{2,1,0:T(8,128)(2,1)S(1)} collective-permute-done((bf16[1,33,2048]{2,1,0:T(8,128)(2,1)S(1)}, bf16[1,33,2048]{2,1,0:T(8,128)(2,1)S(1)}, u32[]{:S(2)}, u32[]{:S(2)}) %collective-permute-start.1) | collective-permute-done | bytes 135200 | tf_op jit(solution)/shard_map/while/body/eval_jaxpr/ppermute | solution.py:12
  429.3 11.2 %conditional.13 = (bf16[1,33,2048]{2,1,0:T(8,128)(2,1)S(1)}, bf16[1,33,2048]{2,1,0:T(8,128)(2,1)S(1)}) conditional(s32[]{:T(128)} %convert_element_type.140, bf16[1,33,2048]{2,1,0:T(8,128)(2,1)S(1)} %get-tuple-element.965, (bf16[1,33,2048]{2,1,0:T(8,128)(2,1)S(1)}, s32[]{:T(128)}, bf16[6,1,33,2048]{3,2,1,0:T(8,128)(2,1)S(1)}, ...), branch_computations={%region_12.12_spmd, %region_13.14_spmd} | conditional | flops 554866688 | bytes 19681334 | solution.py:163
  442.8 15.0 %collective-permute-done.1 = bf16[1,33,2048]{2,1,0:T(8,128)(2,1)S(1)} collective-permute-done((bf16[1,33,2048]{2,1,0:T(8,128)(2,1)S(1)}, bf16[1,33,2048]{2,1,0:T(8,128)(2,1)S(1)}, u32[]{:S(2)}, u32[]{:S(2)}) %collective-permute-start.1) | collective-permute-done | bytes 135200 | tf_op jit(solution)/shard_map/while/body/eval_jaxpr/ppermute | solution.py:12
  458.4 11.2 %conditional.13 = (bf16[1,33,2048]{2,1,0:T(8,128)(2,1)S(1)}, bf16[1,33,2048]{2,1,0:T(8,128)(2,1)S(1)}) conditional(s32[]{:T(128)} %convert_element_type.140, bf16[1,33,2048]{2,1,0:T(8,128)(2,1)S(1)} %get-tuple-element.965, (bf16[1,33,2048]{2,1,0:T(8,128)(2,1)S(1)}, s32[]{:T(128)}, bf16[6,1,33,2048]{3,2,1,0:T(8,128)(2,1)S(1)}, ...), branch_computations={%region_12.12_spmd, %region_13.14_spmd} | conditional | flops 554866688 | bytes 19681334 | solution.py:163
  479.4 48.6 %reduce-scatter.7.cloned.1.call-done = bf16[256,1024]{1,0:T(8,128)(2,1)} async-done(((bf16[2048,1024]{1,0:T(8,128)(2,1)}), bf16[256,1024]{1,0:T(8,128)(2,1)}) %reduce-scatter.7.cloned.1.call-update) | async-done | bytes 524304 | tf_op jit(solution)/shard_map/reduce_scatter | solution.py:197
  535.2 15.4 %psum.15 = bf16[]{:T(256)} all-reduce(f32[]{:T(128)} %get-tuple-element.664), channel_id=1, replica_groups=mesh['dp'=2,'section'=4,'mp'=4] {'dp','mp'}, use_global_device_ids=true, to_apply=%region_21.22 | all-reduce | flops 1 | bytes 6 | tf_op jit(solution)/shard_map/psum | solution.py:203
  551.2 12.1 %all-reduce.1 = bf16[1,4]{1,0:T(2,128)(2,1)S(1)} all-reduce(bf16[1,4]{1,0:T(2,128)(2,1)S(1)} %broadcast_in_dim.72), channel_id=5, replica_groups=mesh['dp'=2,'section'=4,'mp'=4] {'section'}, use_global_device_ids=true, to_apply=%region_22.23.clone | all-reduce | flops 4 | bytes 16
  566.2 59.3 %reduce-scatter.5.cloned.1.call-done = bf16[256,2048]{1,0:T(8,128)(2,1)} async-done(((bf16[2048,2048]{1,0:T(8,128)(2,1)}), bf16[256,2048]{1,0:T(8,128)(2,1)}) %reduce-scatter.5.cloned.1.call-update) | async-done | bytes 1048592 | tf_op jit(solution)/shard_map/reduce_scatter | solution.py:182
  (296 shorter events, 291.1 us)
Async XLA Ops:
  13.1 6.0 copy-start.3
  13.1 104.6 %copy-start.1 = (bf16[512,2048]{1,0:T(8,128)(2,1)S(1)}, bf16[512,2048]{1,0:T(8,128)(2,1)}, u32[]{:S(2)}) copy-start(bf16[512,2048]{1,0:T(8,128)(2,1)} %param.29) | copy-start | bytes 6291460
  13.1 102.7 %all-to-all-start = ((bf16[4,512,2048]{2,1,0:T(8,128)(2,1)}), bf16[4,512,2048]{2,1,0:T(8,128)(2,1)}, u32[]{:S(2)}, u32[]{:S(2)}) async-start(bf16[4,512,2048]{2,1,0:T(8,128)(2,1)} %stack.3), calls=%async_computation | async-start | bytes 16777216 | tf_op jit(solution)/shard_map/all_to_all | solution.py:62
  18.9 509.2 %reduce-scatter.7.cloned.1.call-start = ((), (), s32[]{:S(2)}) async-start(), calls=%async_computation.5 | async-start | bytes 4718592 | tf_op jit(solution)/shard_map/reduce_scatter | solution.py:197
  128.1 4.1 collective-permute-start
  142.7 4.1 collective-permute-start
  157.3 4.1 collective-permute-start
  171.9 4.1 collective-permute-start
  186.5 4.1 collective-permute-start
  201.1 4.1 collective-permute-start
  210.7 7.9 %collective-permute-start = (bf16[1,33,2048]{2,1,0:T(8,128)(2,1)S(1)}, bf16[1,33,2048]{2,1,0:T(8,128)(2,1)}, u32[]{:S(2)}, u32[]{:S(2)}) collective-permute-start(bf16[1,33,2048]{2,1,0:T(8,128)(2,1)S(1)} %get-tuple-element.1090), channel_id=1, source_target_pairs={{0,4},{4,8},{8,12},{1,5},{5,9},{9,13},{2,6},{6,10},{10,14},{3,7},{... | collective-permute-start | bytes 405512 | tf_op jit(solution)/shard_map/while/body/eval_jaxpr/ppermute | solution.py:12
  224.0 4.1 collective-permute-start
  233.5 5.1 collective-permute-start
  239.6 8.3 %collective-permute-start.1 = (bf16[1,33,2048]{2,1,0:T(8,128)(2,1)S(1)}, bf16[1,33,2048]{2,1,0:T(8,128)(2,1)S(1)}, u32[]{:S(2)}, u32[]{:S(2)}) collective-permute-start(bf16[1,33,2048]{2,1,0:T(8,128)(2,1)S(1)} %get-tuple-element.966), channel_id=1, source_target_pairs={{4,0},{8,4},{12,8},{5,1},{9,5},{13,9},{6,2},{10,6},{14,10},{7,3},{... | collective-permute-start | bytes 405512 | tf_op jit(solution)/shard_map/while/body/eval_jaxpr/ppermute | solution.py:12
  248.5 8.8 %collective-permute-start.1 = (bf16[1,33,2048]{2,1,0:T(8,128)(2,1)S(1)}, bf16[1,33,2048]{2,1,0:T(8,128)(2,1)S(1)}, u32[]{:S(2)}, u32[]{:S(2)}) collective-permute-start(bf16[1,33,2048]{2,1,0:T(8,128)(2,1)S(1)} %get-tuple-element.966), channel_id=1, source_target_pairs={{4,0},{8,4},{12,8},{5,1},{9,5},{13,9},{6,2},{10,6},{14,10},{7,3},{... | collective-permute-start | bytes 405512 | tf_op jit(solution)/shard_map/while/body/eval_jaxpr/ppermute | solution.py:12
  258.0 53.9 %collective-permute-start.1 = (bf16[1,33,2048]{2,1,0:T(8,128)(2,1)S(1)}, bf16[1,33,2048]{2,1,0:T(8,128)(2,1)S(1)}, u32[]{:S(2)}, u32[]{:S(2)}) collective-permute-start(bf16[1,33,2048]{2,1,0:T(8,128)(2,1)S(1)} %get-tuple-element.966), channel_id=1, source_target_pairs={{4,0},{8,4},{12,8},{5,1},{9,5},{13,9},{6,2},{10,6},{14,10},{7,3},{... | collective-permute-start | bytes 405512 | tf_op jit(solution)/shard_map/while/body/eval_jaxpr/ppermute | solution.py:12
  323.8 17.3 %collective-permute-start.1 = (bf16[1,33,2048]{2,1,0:T(8,128)(2,1)S(1)}, bf16[1,33,2048]{2,1,0:T(8,128)(2,1)S(1)}, u32[]{:S(2)}, u32[]{:S(2)}) collective-permute-start(bf16[1,33,2048]{2,1,0:T(8,128)(2,1)S(1)} %get-tuple-element.966), channel_id=1, source_target_pairs={{4,0},{8,4},{12,8},{5,1},{9,5},{13,9},{6,2},{10,6},{14,10},{7,3},{... | collective-permute-start | bytes 405512 | tf_op jit(solution)/shard_map/while/body/eval_jaxpr/ppermute | solution.py:12
  353.0 17.3 %collective-permute-start.1 = (bf16[1,33,2048]{2,1,0:T(8,128)(2,1)S(1)}, bf16[1,33,2048]{2,1,0:T(8,128)(2,1)S(1)}, u32[]{:S(2)}, u32[]{:S(2)}) collective-permute-start(bf16[1,33,2048]{2,1,0:T(8,128)(2,1)S(1)} %get-tuple-element.966), channel_id=1, source_target_pairs={{4,0},{8,4},{12,8},{5,1},{9,5},{13,9},{6,2},{10,6},{14,10},{7,3},{... | collective-permute-start | bytes 405512 | tf_op jit(solution)/shard_map/while/body/eval_jaxpr/ppermute | solution.py:12
  382.1 17.3 %collective-permute-start.1 = (bf16[1,33,2048]{2,1,0:T(8,128)(2,1)S(1)}, bf16[1,33,2048]{2,1,0:T(8,128)(2,1)S(1)}, u32[]{:S(2)}, u32[]{:S(2)}) collective-permute-start(bf16[1,33,2048]{2,1,0:T(8,128)(2,1)S(1)} %get-tuple-element.966), channel_id=1, source_target_pairs={{4,0},{8,4},{12,8},{5,1},{9,5},{13,9},{6,2},{10,6},{14,10},{7,3},{... | collective-permute-start | bytes 405512 | tf_op jit(solution)/shard_map/while/body/eval_jaxpr/ppermute | solution.py:12
  411.3 17.3 %collective-permute-start.1 = (bf16[1,33,2048]{2,1,0:T(8,128)(2,1)S(1)}, bf16[1,33,2048]{2,1,0:T(8,128)(2,1)S(1)}, u32[]{:S(2)}, u32[]{:S(2)}) collective-permute-start(bf16[1,33,2048]{2,1,0:T(8,128)(2,1)S(1)} %get-tuple-element.966), channel_id=1, source_target_pairs={{4,0},{8,4},{12,8},{5,1},{9,5},{13,9},{6,2},{10,6},{14,10},{7,3},{... | collective-permute-start | bytes 405512 | tf_op jit(solution)/shard_map/while/body/eval_jaxpr/ppermute | solution.py:12
  440.5 17.3 %collective-permute-start.1 = (bf16[1,33,2048]{2,1,0:T(8,128)(2,1)S(1)}, bf16[1,33,2048]{2,1,0:T(8,128)(2,1)S(1)}, u32[]{:S(2)}, u32[]{:S(2)}) collective-permute-start(bf16[1,33,2048]{2,1,0:T(8,128)(2,1)S(1)} %get-tuple-element.966), channel_id=1, source_target_pairs={{4,0},{8,4},{12,8},{5,1},{9,5},{13,9},{6,2},{10,6},{14,10},{7,3},{... | collective-permute-start | bytes 405512 | tf_op jit(solution)/shard_map/while/body/eval_jaxpr/ppermute | solution.py:12
  469.7 7.2 %collective-permute-start.1 = (bf16[1,33,2048]{2,1,0:T(8,128)(2,1)S(1)}, bf16[1,33,2048]{2,1,0:T(8,128)(2,1)S(1)}, u32[]{:S(2)}, u32[]{:S(2)}) collective-permute-start(bf16[1,33,2048]{2,1,0:T(8,128)(2,1)S(1)} %get-tuple-element.966), channel_id=1, source_target_pairs={{4,0},{8,4},{12,8},{5,1},{9,5},{13,9},{6,2},{10,6},{14,10},{7,3},{... | collective-permute-start | bytes 405512 | tf_op jit(solution)/shard_map/while/body/eval_jaxpr/ppermute | solution.py:12
  479.4 85.2 %reduce-scatter.9.cloned.1.call-start = ((), (), s32[]{:S(2)}) async-start(), calls=%async_computation.6 | async-start | bytes 655360 | tf_op jit(solution)/shard_map/reduce_scatter | solution.py:206
  528.1 97.4 %reduce-scatter.5.cloned.1.call-start = ((), (), s32[]{:S(2)}) async-start(), calls=%async_computation.4 | async-start | bytes 9437184 | tf_op jit(solution)/shard_map/reduce_scatter | solution.py:182
  (2 other events, 6.5 us)
Sparse Core Ops, SparseCore 0:
  479.5 48.5 reduce-scatter.6
  530.3 21.8 reduce-scatter.8
  555.7 69.7 reduce-scatter.4
